TPU v7x, 512 devices: a 4x2x32 block of a 4x8x32 slice. The times are simulated.
512 devices in a mesh: groups: 2 (over y), batch: 128 (over z, x), mp: 2 (over core).
Axes of the slice: x: 4, y: 2, z: 32, core: 2. Of those that a mesh axis runs over, the one named last changes fastest.
The devices are a block of a 4x8x32 slice.
Arguments:
- hidden: bfloat16 [512, 1280], P(('groups', 'batch')), parts along dimension 0, may hold values from -6 to 6
- token_qkv: bfloat16 [3, 512, 1280], P(None, ('groups', 'batch'), 'mp'), parts along dimension 1, may hold values from -6 to 6
- self_cache: bfloat16 [2, 512, 128, 1280], P(None, ('groups', 'batch'), None, 'mp'), parts along dimension 1, may hold values from -6 to 6
- cross_kv: bfloat16 [2, 512, 64, 1280], P(None, ('groups', 'batch'), None, 'mp'), parts along dimension 1, may hold values from -6 to 6
- cache_len: int32 [512], P(('groups', 'batch')), parts along dimension 0, may hold values from 1 to 127
- finished: int32 [512], P(('groups', 'batch')), parts along dimension 0, may hold values 0 or 1
- new_slot: int32 [512], P(('groups', 'batch')), parts along dimension 0, may hold values from 0 to 255, as said below
- out_proj: bfloat16 [1280, 1280], P('mp'), may hold values from -0.15625 to 0.15625
- ln_gain: float32 [1280], replicated, may hold values from 0.5 to 1.5
- ln_bias: float32 [1280], replicated, may hold values from -3 to 3
- query_proj: bfloat16 [1280, 1280], P(None, 'mp'), may hold values from -3 to 3
Outputs:
- moved_cache: bfloat16 [2, 512, 128, 1280], P(None, ('groups', 'batch'), None, 'mp'), parts along dimension 1
- moved_out: bfloat16 [512, 1280], P(('groups', 'batch'), 'mp'), parts along dimension 0
There are 2 independent parts, one for each index of `groups`. A program takes and returns all parts, laid end to end along the dimension named above; an argument that names none is the same for every part. Nothing has to cross between parts.
Inputs may be any that keep to these rules, and one draw needn't show every extreme that they name: A permutation of the spans' slots. Span c's new owner new_slot[c] // 2 lies within 3 devices of its present one c // 2, counting the device order as a loop; of one device's spans at most one moves by any given signed distance.
All inputs are finite; a program needn't handle non-finite values. No bound on the sum of `finished` on one device may be relied on, other than what follows from the above.
Results may differ from a plain program's by a relative error of at most 0.015.
Values may be sent and summed in bfloat16 or wider, within the bound.
No kernel may reach another device: no remote copies, remote signals or barrier semaphores. Data moves between devices by JAX's collectives and lax.ppermute only.
A program may use at most 64 MiB of HBM per device.

v0:
```python
import jax
import jax.numpy as jnp
from jax import lax
from jax.sharding import PartitionSpec as P

HEAD_DIM = 64
REACH = 3


def copy_for_each(array, axis):
    copies = jnp.broadcast_to(array, (lax.axis_size(axis), *array.shape))
    return lax.all_to_all(copies, axis, split_axis=0, concat_axis=0, tiled=True)


def of_everyone(array, axis):
    return copy_for_each(array, axis).sum(axis=0)


def passed_along(block, axis, distance):
    devices = range(lax.axis_size(axis))
    route = [((i - distance) % len(devices), i) for i in devices]
    return lax.ppermute(block, axis, route)


def body(
    hidden,
    token_qkv,
    self_cache,
    cross_kv,
    cache_len,
    finished,
    new_slot,
    out_proj,
    ln_gain,
    ln_bias,
    query_proj,
):
    spans = hidden.shape[0]
    slots = self_cache.shape[2]
    local_width = self_cache.shape[3]
    frames = cross_kv.shape[2]
    head_count = local_width // HEAD_DIM
    factor = HEAD_DIM ** (-0.5)
    new_query = token_qkv[0].reshape(spans, head_count, HEAD_DIM)
    new_key = token_qkv[1].reshape(spans, head_count, HEAD_DIM)
    new_value = token_qkv[2].reshape(spans, head_count, HEAD_DIM)
    cache_keys = self_cache[0].reshape(spans, slots, head_count, HEAD_DIM)
    cache_values = self_cache[1].reshape(spans, slots, head_count, HEAD_DIM)
    scores = (
        jnp.einsum("chd,cthd->cht", new_query, cache_keys, preferred_element_type=jnp.float32)
        * factor
    )
    position = jnp.arange(slots, dtype=jnp.int32)
    usable = position[None, None, :] < cache_len[:, None, None]
    scores = jnp.where(usable, scores, -1e30)
    own_score = (
        jnp.sum(new_query.astype(jnp.float32) * new_key.astype(jnp.float32), axis=-1) * factor
    )
    highest = jnp.maximum(jnp.max(scores, axis=-1), own_score)
    cache_weight = jnp.where(usable, jnp.exp(scores - highest[..., None]), 0.0)
    own_weight = jnp.exp(own_score - highest)
    total = jnp.sum(cache_weight, axis=-1) + own_weight
    cache_weight = (cache_weight / total[..., None]).astype(jnp.bfloat16)
    own_weight = (own_weight / total).astype(jnp.bfloat16)
    context = jnp.einsum(
        "cht,cthd->chd", cache_weight, cache_values, preferred_element_type=jnp.float32
    )
    context = context + own_weight.astype(jnp.float32)[..., None] * new_value.astype(jnp.float32)
    context = context.astype(jnp.bfloat16).reshape(spans, local_width)
    partial_proj = jnp.dot(context, out_proj, preferred_element_type=jnp.float32)
    resid = hidden.astype(jnp.float32) + of_everyone(partial_proj, "mp")
    centre = jnp.mean(resid, axis=-1, keepdims=True)
    spread = jnp.mean((resid - centre) ** 2, axis=-1, keepdims=True)
    normed = ((resid - centre) * lax.rsqrt(spread + 1e-05) * ln_gain + ln_bias).astype(jnp.bfloat16)
    cross_query = jnp.dot(normed, query_proj, preferred_element_type=jnp.float32).astype(
        jnp.bfloat16
    )
    cross_query = cross_query.reshape(spans, head_count, HEAD_DIM)
    cross_keys = cross_kv[0].reshape(spans, frames, head_count, HEAD_DIM)
    cross_values = cross_kv[1].reshape(spans, frames, head_count, HEAD_DIM)
    cross_scores = (
        jnp.einsum("chd,cthd->cht", cross_query, cross_keys, preferred_element_type=jnp.float32)
        * factor
    )
    cross_high = jnp.max(cross_scores, axis=-1, keepdims=True)
    cross_exp = jnp.exp(cross_scores - cross_high)
    cross_weight = (cross_exp / jnp.sum(cross_exp, axis=-1, keepdims=True)).astype(jnp.bfloat16)
    cross_context = jnp.einsum(
        "cht,cthd->chd", cross_weight, cross_values, preferred_element_type=jnp.float32
    )
    cross_context = cross_context.reshape(spans, local_width)
    alive = finished == 0
    decoded = jnp.where(alive[:, None], cross_context, 0.0).astype(jnp.bfloat16)
    slot_pos = position[None, :, None]
    length = cache_len[:, None, None]

    def extend(older, fresh):
        grown = jnp.where(
            slot_pos < length,
            older,
            jnp.where(slot_pos == length, fresh[:, None, :], jnp.zeros_like(older)),
        )
        return jnp.where(alive[:, None, None], grown, jnp.zeros_like(older))

    updated = jnp.stack([extend(self_cache[0], token_qkv[1]), extend(self_cache[1], token_qkv[2])])
    device_index = lax.axis_index("batch")
    device_count = lax.axis_size("batch")
    dest_device = new_slot // spans
    dest_local = new_slot % spans
    half_count = device_count // 2
    offset = (dest_device - device_index + half_count) % device_count - half_count
    placing = dest_local[:, None] == jnp.arange(spans, dtype=jnp.int32)[None, :]
    select = ((offset == 0)[:, None] & placing).astype(jnp.bfloat16)
    cache_part = jnp.einsum("jl,ajtd->altd", select, updated, preferred_element_type=jnp.float32)
    out_part = jnp.einsum("jl,jd->ld", select, decoded, preferred_element_type=jnp.float32)
    cache_total = cache_part
    out_total = out_part
    distances = [shift_by for shift_by in range(-REACH, REACH + 1) if shift_by != 0]
    placing_weights = placing.astype(jnp.bfloat16)
    for distance in distances:
        picked = (offset == distance).astype(jnp.bfloat16)
        payload = jnp.einsum(
            "j,ajtd->atd", picked, updated, preferred_element_type=jnp.float32
        ).astype(jnp.bfloat16)
        out_row = jnp.einsum("j,jd->d", picked, decoded, preferred_element_type=jnp.float32).astype(
            jnp.bfloat16
        )
        marker = jnp.einsum(
            "j,jl->l", picked, placing_weights, preferred_element_type=jnp.float32
        ).astype(jnp.bfloat16)
        marker_row = jnp.pad(marker, (0, local_width - spans))
        parcel = jnp.concatenate(
            [payload.reshape(2 * slots, local_width), out_row[None, :], marker_row[None, :]], 0
        )
        arrived = passed_along(parcel, "batch", distance)
        got_cache = arrived[: 2 * slots].reshape(2, slots, local_width)
        got_out = arrived[2 * slots]
        got_marker = arrived[2 * slots + 1, :spans]
        cache_total = cache_total + jnp.einsum(
            "l,atd->altd", got_marker, got_cache, preferred_element_type=jnp.float32
        )
        out_total = out_total + jnp.einsum(
            "l,d->ld", got_marker, got_out, preferred_element_type=jnp.float32
        )
    return (cache_total.astype(jnp.bfloat16), out_total.astype(jnp.bfloat16))


def solution(mesh):
    placed = (
        P(("groups", "batch"), None),
        P(None, ("groups", "batch"), "mp"),
        P(None, ("groups", "batch"), None, "mp"),
        P(None, ("groups", "batch"), None, "mp"),
        P(("groups", "batch")),
        P(("groups", "batch")),
        P(("groups", "batch")),
        P("mp", None),
        P(),
        P(),
        P(None, "mp"),
    )
    return jax.shard_map(
        body,
        mesh=mesh,
        in_specs=placed,
        out_specs=(P(None, ("groups", "batch"), None, "mp"), P(("groups", "batch"), "mp")),
        check_vma=False,
    )
```

profile of v0, /device:TPU:33, one launch (start us, length us, event | category | flops | bytes accessed | tf_op | source)
XLA Modules:
  0.0 109.1 jit_solution(13605991024664097077)
XLA Ops:
  0.6 0.8 slice_bitcast_fusion.1
  2.6 1.2 %fusion.108 = (bf16[1,2,128,640]{3,2,1,0:T(8,128)(2,1)S(1)}, bf16[1,2,128,640]{3,2,1,0:T(8,128)(2,1)S(1)}) fusion(bf16[2,2,128,640]{3,2,1,0:T(8,128)(2,1)} %param.13), kind=kLoop, calls=%fused_computation.188 | loop fusion | bytes 1310720 | tf_op jit(solution)/shard_map/slice | solution.py:105
  6.7 44.7 %all-to-all-start = ((f32[2,2,1280]{2,1,0:T(2,128)}), f32[2,2,1280]{2,1,0:T(2,128)S(1)}, u32[]{:S(2)}, u32[]{:S(2)}) async-start(f32[2,2,1280]{2,1,0:T(2,128)} %broadcast_in_dim.149), calls=%async_computation | async-start | bytes 40960 | tf_op jit(solution)/shard_map/all_to_all | solution.py:12
  52.8 1.8 %convolution_convert_fusion = bf16[2,640]{1,0:T(2,128)(2,1)S(1)} fusion(bf16[1280,640]{1,0:T(8,128)(2,1)} %param.21, f32[2]{0:T(128)S(1)} %add_rsqrt_fusion, f32[2]{0:T(128)S(1)} %broadcast_multiply_fusion, f32[1280]{0:T(1024)S(1)} %copy-done.3, f32[1280]{0:T(1024)S(1)} %copy-done.4, f32[2,1280]{1,0:T(2,128)S(1)} %reduce_sum.56, ...), kind=kOutput, calls=%fused_computation.8 | convolution fusion | flops 3296000 | bytes 1666576 | tf_op jit(solution)/shard_map/dot_general | solution.py:75
  55.7 1.4 %broadcast_select_fusion.5 = (bf16[1,2,128,640]{3,1,2,0:T(2,128)(2,1)S(1)}, bf16[1,2,128,640]{3,1,2,0:T(2,128)(2,1)S(1)}) fusion(pred[2]{0:T(512)(128)(4,1)S(1)} %broadcast_compare_fusion.7, pred[2,128]{0,1:T(8,128)(4,1)S(1)} %get-tuple-element.30, pred[2,128]{0,1:T(8,128)(4,1)S(1)} %get-tuple-element.29, bf16[1,2,128,640]{3,2,1,0:T(8,128)(2,1)S(1)} %get-tuple-element.16, ...), kind=kLoop, calls=%fused_computation.39 | loop fusion | flops 983040 | bytes 1316354 | tf_op jit(solution)/shard_map/jit(_where)/select_n | solution.py:103
  57.1 0.9 pad_maximum_fusion
  58.1 0.8 fusion.49
  59.0 2.0 %collective-permute-start.5 = (bf16[258,640]{1,0:T(8,128)(2,1)S(1)}, bf16[258,640]{1,0:T(8,128)(2,1)S(1)}, u32[]{:S(2)}, u32[]{:S(2)}) collective-permute-start(bf16[258,640]{1,0:T(8,128)(2,1)S(1)} %pad_maximum_fusion.6), channel_id=1, source_target_pairs={{250,0},{252,2},{254,4},{0,6},{2,8},{4,10},{6,12},{8,14},{10,16},{... | collective-permute-start | bytes 990728 | tf_op jit(solution)/shard_map/ppermute | solution.py:22
  61.2 0.8 fusion.51
  62.2 2.0 %collective-permute-start.4 = (bf16[258,640]{1,0:T(8,128)(2,1)S(1)}, bf16[258,640]{1,0:T(8,128)(2,1)S(1)}, u32[]{:S(2)}, u32[]{:S(2)}) collective-permute-start(bf16[258,640]{1,0:T(8,128)(2,1)S(1)} %pad_maximum_fusion.5), channel_id=1, source_target_pairs={{252,0},{254,2},{0,4},{2,6},{4,8},{6,10},{8,12},{10,14},{12,16},{1... | collective-permute-start | bytes 990728 | tf_op jit(solution)/shard_map/ppermute | solution.py:22
  64.4 0.8 fusion.53
  65.4 2.0 %collective-permute-start.3 = (bf16[258,640]{1,0:T(8,128)(2,1)S(1)}, bf16[258,640]{1,0:T(8,128)(2,1)S(1)}, u32[]{:S(2)}, u32[]{:S(2)}) collective-permute-start(bf16[258,640]{1,0:T(8,128)(2,1)S(1)} %pad_maximum_fusion.4), channel_id=1, source_target_pairs={{254,0},{0,2},{2,4},{4,6},{6,8},{8,10},{10,12},{12,14},{14,16},{16... | collective-permute-start | bytes 990728 | tf_op jit(solution)/shard_map/ppermute | solution.py:22
  67.6 0.8 fusion.55
  68.5 7.7 %collective-permute-start.2 = (bf16[258,640]{1,0:T(8,128)(2,1)S(1)}, bf16[258,640]{1,0:T(8,128)(2,1)S(1)}, u32[]{:S(2)}, u32[]{:S(2)}) collective-permute-start(bf16[258,640]{1,0:T(8,128)(2,1)S(1)} %pad_maximum_fusion.3), channel_id=1, source_target_pairs={{2,0},{4,2},{6,4},{8,6},{10,8},{12,10},{14,12},{16,14},{18,16},{20... | collective-permute-start | bytes 990728 | tf_op jit(solution)/shard_map/ppermute | solution.py:22
  76.5 0.8 fusion.57
  77.4 4.3 %collective-permute-start.1 = (bf16[258,640]{1,0:T(8,128)(2,1)S(1)}, bf16[258,640]{1,0:T(8,128)(2,1)S(1)}, u32[]{:S(2)}, u32[]{:S(2)}) collective-permute-start(bf16[258,640]{1,0:T(8,128)(2,1)S(1)} %pad_maximum_fusion.2), channel_id=1, source_target_pairs={{4,0},{6,2},{8,4},{10,6},{12,8},{14,10},{16,12},{18,14},{20,16},{2... | collective-permute-start | bytes 990728 | tf_op jit(solution)/shard_map/ppermute | solution.py:22
  82.0 0.8 fusion.59
  83.0 4.3 %collective-permute-start = (bf16[258,640]{1,0:T(8,128)(2,1)S(1)}, bf16[258,640]{1,0:T(8,128)(2,1)S(1)}, u32[]{:S(2)}, u32[]{:S(2)}) collective-permute-start(bf16[258,640]{1,0:T(8,128)(2,1)S(1)} %pad_maximum_fusion.1), channel_id=1, source_target_pairs={{6,0},{8,2},{10,4},{12,6},{14,8},{16,10},{18,12},{20,14},{22,16},{... | collective-permute-start | bytes 990728 | tf_op jit(solution)/shard_map/ppermute | solution.py:22
  87.5 2.2 %collective-permute-done.3 = bf16[258,640]{1,0:T(8,128)(2,1)S(1)} collective-permute-done((bf16[258,640]{1,0:T(8,128)(2,1)S(1)}, bf16[258,640]{1,0:T(8,128)(2,1)S(1)}, u32[]{:S(2)}, u32[]{:S(2)}) %collective-permute-start.3) | collective-permute-done | bytes 330272 | tf_op jit(solution)/shard_map/ppermute | solution.py:22
  89.9 7.6 %collective-permute-done.1 = bf16[258,640]{1,0:T(8,128)(2,1)S(1)} collective-permute-done((bf16[258,640]{1,0:T(8,128)(2,1)S(1)}, bf16[258,640]{1,0:T(8,128)(2,1)S(1)}, u32[]{:S(2)}, u32[]{:S(2)}) %collective-permute-start.1) | collective-permute-done | bytes 330272 | tf_op jit(solution)/shard_map/ppermute | solution.py:22
  97.6 6.4 %collective-permute-done = bf16[258,640]{1,0:T(8,128)(2,1)S(1)} collective-permute-done((bf16[258,640]{1,0:T(8,128)(2,1)S(1)}, bf16[258,640]{1,0:T(8,128)(2,1)S(1)}, u32[]{:S(2)}, u32[]{:S(2)}) %collective-permute-start) | collective-permute-done | bytes 330272 | tf_op jit(solution)/shard_map/ppermute | solution.py:22
  104.2 3.1 %fusion.13 = bf16[2,2,128,640]{3,1,2,0:T(2,128)(2,1)S(1)} fusion(f32[2]{0:T(128)S(1)} %fusion.70, f32[2,128,640]{2,1,0:T(8,128)S(1)} %convert.145, f32[2]{0:T(128)S(1)} %fusion.71, f32[2,128,640]{2,1,0:T(8,128)S(1)} %convert.144, f32[2]{0:T(128)S(1)} %fusion.72, f32[2,128,640]{2,1,0:T(8,128)S(1)} %convert.143, f32[2]{0:T(128)S(1)} %fusion.73, ...), kind=kOutput, calls=%fused_computation.40 | convolution fusion | flops 5570568 | bytes 5242938 | tf_op jit(solution)/shard_map/jl,ajtd->altd/dot_general | solution.py:114
  107.3 0.9 copy.55
  108.4 0.7 add_convert_fusion.3
  (126 shorter events, 8.9 us)
Async XLA Ops:
  0.6 5.1 %copy-start = (bf16[640,1280]{1,0:T(8,128)(2,1)S(1)}, bf16[640,1280]{1,0:T(8,128)(2,1)}, u32[]{:S(2)}) copy-start(bf16[640,1280]{1,0:T(8,128)(2,1)} %param.18) | copy-start | bytes 4915204
  4.9 46.4 %copy-start.5 = (s32[2]{0:T(128)S(1)}, s32[2]{0:T(128)}, u32[]{:S(2)}) copy-start(s32[2]{0:T(128)} %param.17) | copy-start | bytes 28
  4.9 46.4 %copy-start.6 = (s32[2]{0:T(128)S(1)}, s32[2]{0:T(128)}, u32[]{:S(2)}) copy-start(s32[2]{0:T(128)} %param.16) | copy-start | bytes 28
  4.9 46.6 %copy-start.1 = (bf16[2,2,64,640]{3,2,1,0:T(8,128)(2,1)S(1)}, bf16[2,2,64,640]{3,2,1,0:T(8,128)(2,1)}, u32[]{:S(2)}) copy-start(bf16[2,2,64,640]{3,2,1,0:T(8,128)(2,1)} %param.14) | copy-start | bytes 983044
  5.7 46.7 %copy-start.2 = (bf16[2,1280]{1,0:T(2,128)(2,1)S(1)}, bf16[2,1280]{1,0:T(2,128)(2,1)}, u32[]{:S(2)}) copy-start(bf16[2,1280]{1,0:T(2,128)(2,1)} %param.11) | copy-start | bytes 15364
  6.0 46.7 %copy-start.3 = (f32[1280]{0:T(1024)S(1)}, f32[1280]{0:T(1024)}, u32[]{:S(2)}) copy-start(f32[1280]{0:T(1024)} %param.20) | copy-start | bytes 15364
  6.0 46.7 %copy-start.4 = (f32[1280]{0:T(1024)S(1)}, f32[1280]{0:T(1024)}, u32[]{:S(2)}) copy-start(f32[1280]{0:T(1024)} %param.19) | copy-start | bytes 15364
  6.7 45.7 %all-to-all-start = ((f32[2,2,1280]{2,1,0:T(2,128)}), f32[2,2,1280]{2,1,0:T(2,128)S(1)}, u32[]{:S(2)}, u32[]{:S(2)}) async-start(f32[2,2,1280]{2,1,0:T(2,128)} %broadcast_in_dim.149), calls=%async_computation | async-start | bytes 40960 | tf_op jit(solution)/shard_map/all_to_all | solution.py:12
  59.0 24.0 %collective-permute-start.5 = (bf16[258,640]{1,0:T(8,128)(2,1)S(1)}, bf16[258,640]{1,0:T(8,128)(2,1)S(1)}, u32[]{:S(2)}, u32[]{:S(2)}) collective-permute-start(bf16[258,640]{1,0:T(8,128)(2,1)S(1)} %pad_maximum_fusion.6), channel_id=1, source_target_pairs={{250,0},{252,2},{254,4},{0,6},{2,8},{4,10},{6,12},{8,14},{10,16},{... | collective-permute-start | bytes 990728 | tf_op jit(solution)/shard_map/ppermute | solution.py:22
  62.2 25.2 %collective-permute-start.4 = (bf16[258,640]{1,0:T(8,128)(2,1)S(1)}, bf16[258,640]{1,0:T(8,128)(2,1)S(1)}, u32[]{:S(2)}, u32[]{:S(2)}) collective-permute-start(bf16[258,640]{1,0:T(8,128)(2,1)S(1)} %pad_maximum_fusion.5), channel_id=1, source_target_pairs={{252,0},{254,2},{0,4},{2,6},{4,8},{6,10},{8,12},{10,14},{12,16},{1... | collective-permute-start | bytes 990728 | tf_op jit(solution)/shard_map/ppermute | solution.py:22
  65.4 24.3 %collective-permute-start.3 = (bf16[258,640]{1,0:T(8,128)(2,1)S(1)}, bf16[258,640]{1,0:T(8,128)(2,1)S(1)}, u32[]{:S(2)}, u32[]{:S(2)}) collective-permute-start(bf16[258,640]{1,0:T(8,128)(2,1)S(1)} %pad_maximum_fusion.4), channel_id=1, source_target_pairs={{254,0},{0,2},{2,4},{4,6},{6,8},{8,10},{10,12},{12,14},{14,16},{16... | collective-permute-start | bytes 990728 | tf_op jit(solution)/shard_map/ppermute | solution.py:22
  68.5 21.2 %collective-permute-start.2 = (bf16[258,640]{1,0:T(8,128)(2,1)S(1)}, bf16[258,640]{1,0:T(8,128)(2,1)S(1)}, u32[]{:S(2)}, u32[]{:S(2)}) collective-permute-start(bf16[258,640]{1,0:T(8,128)(2,1)S(1)} %pad_maximum_fusion.3), channel_id=1, source_target_pairs={{2,0},{4,2},{6,4},{8,6},{10,8},{12,10},{14,12},{16,14},{18,16},{20... | collective-permute-start | bytes 990728 | tf_op jit(solution)/shard_map/ppermute | solution.py:22
  77.4 20.1 %collective-permute-start.1 = (bf16[258,640]{1,0:T(8,128)(2,1)S(1)}, bf16[258,640]{1,0:T(8,128)(2,1)S(1)}, u32[]{:S(2)}, u32[]{:S(2)}) collective-permute-start(bf16[258,640]{1,0:T(8,128)(2,1)S(1)} %pad_maximum_fusion.2), channel_id=1, source_target_pairs={{4,0},{6,2},{8,4},{10,6},{12,8},{14,10},{16,12},{18,14},{20,16},{2... | collective-permute-start | bytes 990728 | tf_op jit(solution)/shard_map/ppermute | solution.py:22
  83.0 21.1 %collective-permute-start = (bf16[258,640]{1,0:T(8,128)(2,1)S(1)}, bf16[258,640]{1,0:T(8,128)(2,1)S(1)}, u32[]{:S(2)}, u32[]{:S(2)}) collective-permute-start(bf16[258,640]{1,0:T(8,128)(2,1)S(1)} %pad_maximum_fusion.1), channel_id=1, source_target_pairs={{6,0},{8,2},{10,4},{12,6},{14,8},{16,10},{18,12},{20,14},{22,16},{... | collective-permute-start | bytes 990728 | tf_op jit(solution)/shard_map/ppermute | solution.py:22
where the time goes:
time: 109 us
  starting transfers between devices  66.8 us (61%)
  waiting for transfers between devices  16.7 us (15%)
  matrix products  13.4 us (12%)
  other arithmetic  5.71 us (5%)
  local copies, waits for them, and re-layouts  5.24 us (5%)
  between operations  1.27 us (1%)
    all_to_all x1, starting transfers between devices, copy_for_each(): return lax.all_to_all(copies, axis, split_axis=0, concat_axis=0, tiled=True)  44.7 us
    ppermute x6, starting transfers between devices, passed_along(): return lax.ppermute(block, axis, route)  22.1 us
    ppermute x6, waiting for transfers between devices, passed_along(): return lax.ppermute(block, axis, route)  16.3 us
    dot_general x6, matrix products, body(): jnp.einsum('j,ajtd->atd', picked, updated, preferred_element_type=jnp.flo...  4.96 us
    dot_general x1, matrix products, body(): jnp.einsum('jl,ajtd->altd', select, updated, preferred_element_type=jnp.f...  3.13 us
  transfers between devices with their start and end apart: 7, of which 4 were waited for; matrix products, arithmetic and copies ran while one was open for 6% of the time, Pallas kernels for 0%

commit v1 on v0

v1 whole, which is shorter than its diff:
```python
import collections
import functools

import jax
import jax.numpy as jnp
from jax import lax
from jax.experimental import pallas as pl
from jax.experimental.pallas import tpu as pltpu
from jax.sharding import PartitionSpec as P


HEAD_DIM = 64
RING = 4
SHIFT = 2
TAIL = 8

LIMIT = pltpu.CompilerParams(vmem_limit_bytes=12 * 2**20)
VMEM = pl.BlockSpec(memory_space=pltpu.VMEM)
SMEM = pl.BlockSpec(memory_space=pltpu.SMEM)
HBM = pl.BlockSpec(memory_space=pltpu.HBM)
ANY = pl.BlockSpec(memory_space=pl.ANY)


Plan = collections.namedtuple("Plan", ("local", "stays", "inside", "outside", "place", "turn"))


def moves(new_slot, me, spans, count, j):
    slot = new_slot[j]
    dest = (slot // spans + SHIFT) % count
    mine = (me + SHIFT) % count
    stays = dest == mine
    inside = (dest // RING == mine // RING) & ~stays
    place = dest % RING
    turn = (place - mine % RING + RING) % RING
    return Plan(slot % spans, stays, inside, ~stays & ~inside, place, turn)


def prepare(me_hbm, length_hbm, finished_hbm, slot_hbm, qkv_hbm, cache_hbm, *rest, count):
    updated, chunks, me_ref, length, finished, new_slot, qkv, cache, sems = rest
    pairs = (
        (cache_hbm, cache),
        (me_hbm, me_ref),
        (length_hbm, length),
        (finished_hbm, finished),
        (slot_hbm, new_slot),
        (qkv_hbm, qkv),
    )
    copies = [pltpu.make_async_copy(a, b, sems.at[i]) for i, (a, b) in enumerate(pairs)]
    for copy in copies:
        copy.start()
    for copy in copies:
        copy.wait()
    spans, slots, width = cache.shape[1:]
    me = me_ref[0]
    position = lax.broadcasted_iota(jnp.int32, (slots, width), 0)
    sends = []
    for j in range(spans):
        limit = jnp.where(finished[j] == 0, length[j], -1)
        for a in range(2):
            older = cache[a, j].astype(jnp.float32)
            fresh = qkv[a + 1, j : j + 1].astype(jnp.float32)
            grown = jnp.where(position < limit, older, jnp.where(position == limit, fresh, 0.0))
            updated[j, a * slots : (a + 1) * slots] = grown.astype(jnp.bfloat16)
        plan = moves(new_slot, me, spans, count, j)
        send = pltpu.make_async_copy(updated.at[j], chunks.at[plan.place], sems.at[j])
        sends.append((plan.inside, send))

        @pl.when(plan.inside)
        def _(send=send):
            send.start()

    for inside, send in sends:

        @pl.when(inside)
        def _(send=send):
            send.wait()


def pick(plans, wanted, lines):
    mark = jnp.int32(0)
    line = jnp.zeros_like(lines[0])
    for plan, chosen, candidate in zip(plans, wanted, lines, strict=True):
        mark = jnp.where(chosen, plan.local + 1, mark)
        line = jnp.where(chosen, candidate, line)
    return line, mark.astype(jnp.float32)


def tile_of(line, mark):
    shape = (TAIL, line.shape[1])
    first = lax.broadcasted_iota(jnp.int32, shape, 0) == 0
    return jnp.where(first, jnp.broadcast_to(line, shape), mark).astype(jnp.bfloat16)


def head_rows(row, heads, width):
    head = lax.broadcasted_iota(jnp.int32, (heads, width), 0)
    column = lax.broadcasted_iota(jnp.int32, (heads, width), 1)
    own = column // HEAD_DIM == head
    return own, jnp.where(own, jnp.broadcast_to(row, (heads, width)), 0.0)


def self_attention(length, qkv, cache, proj_hbm, partial, proj, sem):
    copy = pltpu.make_async_copy(proj_hbm, proj, sem)
    copy.start()
    spans, _, width = cache.shape[1:]
    heads = -(-(width // HEAD_DIM) // 8) * 8
    factor = HEAD_DIM ** (-0.5)
    contexts = []
    for j in range(spans):
        query, key, value = (qkv[i, j : j + 1].astype(jnp.float32) for i in range(3))
        own, query_rows = head_rows(query, heads, width)
        scores = (
            lax.dot_general(
                query_rows.astype(jnp.bfloat16), cache[0, j], (((1,), (1,)), ((), ())), preferred_element_type=jnp.float32
            )
            * factor
        )
        usable = lax.broadcasted_iota(jnp.int32, scores.shape, 1) < length[j]
        scores = jnp.where(usable, scores, -1e30)
        own_score = jnp.sum(query_rows * key, axis=1, keepdims=True) * factor
        highest = jnp.maximum(jnp.max(scores, axis=1, keepdims=True), own_score)
        weight = jnp.where(usable, jnp.exp(scores - highest), 0.0)
        own_weight = jnp.exp(own_score - highest)
        total = jnp.sum(weight, axis=1, keepdims=True) + own_weight
        weight = (weight / total).astype(jnp.bfloat16)
        own_weight = (own_weight / total).astype(jnp.bfloat16).astype(jnp.float32)
        mixed = jnp.dot(weight, cache[1, j], preferred_element_type=jnp.float32) + own_weight * value
        contexts.append(jnp.sum(jnp.where(own, mixed, 0.0), axis=0, keepdims=True))
    context = jnp.concatenate(contexts, axis=0).astype(jnp.bfloat16)
    copy.wait()
    partial[...] = jnp.dot(context, proj[...], preferred_element_type=jnp.float32)


def cross_attention(
    me_ref, finished, new_slot, hidden, mine, other, gain, bias, cross, updated, proj_hbm, decoded, near, far1, far2, far3, proj, sem, *, count
):
    copy = pltpu.make_async_copy(proj_hbm, proj, sem)
    copy.start()
    spans, _, width = cross.shape[1:]
    rows = updated.shape[1]
    heads = -(-(width // HEAD_DIM) // 8) * 8
    factor = HEAD_DIM ** (-0.5)
    plans = [moves(new_slot, me_ref[0], spans, count, j) for j in range(spans)]
    parcels = [(block, [p.outside & (p.turn == k) for p in plans]) for k, block in enumerate((far1, far2, far3), 1)]
    for block, wanted in parcels:
        for j, chosen in enumerate(wanted):

            @pl.when(chosen)
            def _(j=j, block=block):
                block[:rows] = updated[j]

    resid = hidden[...].astype(jnp.float32) + (mine[...] + other[...])
    centre = jnp.mean(resid, axis=1, keepdims=True)
    spread = jnp.mean((resid - centre) ** 2, axis=1, keepdims=True)
    normed = ((resid - centre) * lax.rsqrt(spread + 1e-05) * gain[...][None] + bias[...][None]).astype(jnp.bfloat16)
    copy.wait()
    queries = jnp.dot(normed, proj[...], preferred_element_type=jnp.float32).astype(jnp.bfloat16).astype(jnp.float32)
    results = []
    for j in range(spans):
        own, query_rows = head_rows(queries[j : j + 1], heads, width)
        scores = (
            lax.dot_general(
                query_rows.astype(jnp.bfloat16), cross[0, j], (((1,), (1,)), ((), ())), preferred_element_type=jnp.float32
            )
            * factor
        )
        weight = jnp.exp(scores - jnp.max(scores, axis=1, keepdims=True))
        weight = (weight / jnp.sum(weight, axis=1, keepdims=True)).astype(jnp.bfloat16)
        mixed = jnp.dot(weight, cross[1, j], preferred_element_type=jnp.float32)
        result = jnp.sum(jnp.where(own, mixed, 0.0), axis=0, keepdims=True)
        results.append(jnp.where(finished[j] == 0, result, 0.0))
    decoded[...] = jnp.concatenate(results, axis=0).astype(jnp.bfloat16)
    for block, wanted in parcels:
        block[rows:] = tile_of(*pick(plans, wanted, results))
    for x in range(RING):
        near[x] = tile_of(*pick(plans, [p.inside & (p.place == x) for p in plans], results))


def assemble(me_ref, new_slot, updated, decoded, inner, near, got1, got2, got3, moved, moved_out, *, count):
    spans, slots, width = moved.shape[1:]
    rows = 2 * slots
    me = me_ref[0]
    sources = []
    tails = [(near[x], inner.at[x]) for x in range(RING)] + [(got[rows:], got) for got in (got1, got2, got3)]
    for tile, block in tails:
        tile = tile.astype(jnp.float32)
        sources.append((jnp.max(tile[1:, :128]), block, tile[:1]))
    for j in range(spans):
        p = moves(new_slot, me, spans, count, j)
        mark = jnp.where(p.stays, p.local + 1, 0).astype(jnp.float32)
        sources.append((mark, updated.at[j], decoded[j : j + 1].astype(jnp.float32)))
    for l in range(spans):
        row = jnp.zeros((1, width), jnp.float32)
        for mark, block, line in sources:
            chosen = mark == l + 1
            row = jnp.where(chosen, line, row)

            @pl.when(chosen)
            def _(block=block, l=l):
                for a in range(2):
                    moved[a, l] = block[a * slots : (a + 1) * slots]

        moved_out[l : l + 1] = row.astype(jnp.bfloat16)


def here(array):
    return pltpu.with_memory_space_constraint(array, pltpu.VMEM)


def there(array):
    return pltpu.with_memory_space_constraint(array, pltpu.HBM)


def body(hidden, token_qkv, self_cache, cross_kv, cache_len, finished, new_slot, out_proj, ln_gain, ln_bias, query_proj):
    spans, slots, width = self_cache.shape[1:]
    rows = 2 * slots
    count = lax.axis_size("batch")
    cores = lax.axis_size("mp")
    me = lax.axis_index("batch").astype(jnp.int32).reshape(1)
    rings = [[(r * RING + i - SHIFT) % count for i in range(RING)] for r in range(count // RING)]
    bf16 = jnp.bfloat16

    def exchange(chunks):
        return here(lax.all_to_all(chunks, "batch", split_axis=0, concat_axis=0, tiled=True, axis_index_groups=rings))

    def route(k):
        pairs = []
        for i in range(count):
            ring, x = divmod((i + SHIFT) % count, RING)
            to = (x + k) % RING
            pairs.append((i, ((ring + (1 if to < x else -1)) * RING + to - SHIFT) % count))
        return pairs

    block = pltpu.VMEM((rows + TAIL, width), bf16)
    updated, chunks = pl.pallas_call(
        functools.partial(prepare, count=count),
        in_specs=[HBM] * 6,
        out_specs=[VMEM, HBM],
        out_shape=[pltpu.VMEM((spans, rows, width), bf16), pltpu.HBM((RING, rows, width), bf16)],
        scratch_shapes=[pltpu.SMEM((1,), jnp.int32)]
        + [pltpu.SMEM((spans,), jnp.int32)] * 3
        + [pltpu.VMEM(token_qkv.shape, bf16), pltpu.VMEM(self_cache.shape, bf16), pltpu.SemaphoreType.DMA((6,))],
        compiler_params=LIMIT,
        name="prepare",
    )(*map(there, (me, cache_len, finished, new_slot, token_qkv, self_cache)))
    inner = exchange(chunks)
    partial = pl.pallas_call(
        self_attention,
        in_specs=[SMEM, VMEM, VMEM, HBM],
        out_specs=VMEM,
        out_shape=pltpu.VMEM((spans, out_proj.shape[1]), jnp.float32),
        scratch_shapes=[pltpu.VMEM(out_proj.shape, bf16), pltpu.SemaphoreType.DMA],
        compiler_params=LIMIT,
        name="self_attention",
    )(cache_len, token_qkv, self_cache, there(out_proj))
    other = here(lax.ppermute(partial, "mp", [(i, (i + 1) % cores) for i in range(cores)]))
    decoded, near, *far = pl.pallas_call(
        functools.partial(cross_attention, count=count),
        in_specs=[SMEM] * 3 + [VMEM] * 7 + [HBM],
        out_specs=[VMEM] * 5,
        out_shape=[pltpu.VMEM((spans, width), bf16), pltpu.VMEM((RING, TAIL, width), bf16)] + [block] * 3,
        scratch_shapes=[pltpu.VMEM(query_proj.shape, bf16), pltpu.SemaphoreType.DMA],
        compiler_params=LIMIT,
        name="cross_attention",
    )(me, finished, new_slot, hidden, here(partial), other, ln_gain, ln_bias, cross_kv, here(updated), there(query_proj))
    got = []
    for k, sent in enumerate(far, 1):
        got.append(here(lax.ppermute(sent, "batch", route(k))))
    close = exchange(near)
    return pl.pallas_call(
        functools.partial(assemble, count=count),
        in_specs=[SMEM] * 2 + [VMEM] * 7,
        out_specs=[VMEM] * 2,
        out_shape=[jax.ShapeDtypeStruct(self_cache.shape, bf16), jax.ShapeDtypeStruct((spans, width), bf16)],
        compiler_params=LIMIT,
        name="assemble",
    )(me, new_slot, here(updated), here(decoded), inner, close, *got)


def solution(mesh):
    placed = (
        P(("groups", "batch"), None),
        P(None, ("groups", "batch"), "mp"),
        P(None, ("groups", "batch"), None, "mp"),
        P(None, ("groups", "batch"), None, "mp"),
        P(("groups", "batch")),
        P(("groups", "batch")),
        P(("groups", "batch")),
        P("mp", None),
        P(),
        P(),
        P(None, "mp"),
    )

    return jax.shard_map(
        body,
        mesh=mesh,
        in_specs=placed,
        out_specs=(P(None, ("groups", "batch"), None, "mp"), P(("groups", "batch"), "mp")),
        check_vma=False,
    )
```

time: 109 us -> 105 us (0.963)
  matrix products: 13.4 us -> 0 us
  Pallas kernels: 0 us -> 10 us
  blocking collectives: 0 us -> 9.31 us
  starting transfers between devices: 66.8 us -> 60 us
  other arithmetic: 5.71 us -> 0 us
  waiting for transfers between devices: 16.7 us -> 21.6 us
  local copies, waits for them, and re-layouts: 5.24 us -> 2.46 us
    all_to_all x1, starting transfers between devices: 44.7 us -> 8.17 us  [exchange(): lax.all_to_all(chunks, 'batch', split_axis=0, concat_axis=0, tiled=True,...]
    ppermute x6 -> x4, starting transfers between devices: 22.1 us -> 51.9 us  [the longest x1 43.4 us: body(): lax.ppermute(partial, 'mp', [(i, (i + 1) % cores) for i in range(cores)])]
    dot_general x26 -> x0, matrix products: 13.4 us -> none  [the longest x6 4.96 us: body(): jnp.einsum('j,ajtd->atd', picked, updated, preferred_element_type=jnp.flo...]
    pallas_call x0 -> x4, Pallas kernels: none -> 10 us  [the longest x1 3.93 us: body(): pl.pallas_call(functools.partial(cross_attention, count=count), in_specs=...]
    all_to_all x0 -> x1, blocking collectives: none -> 9.31 us  [exchange(): lax.all_to_all(chunks, 'batch', split_axis=0, concat_axis=0, tiled=True,...]
    ppermute x6 -> x4, waiting for transfers between devices: 16.3 us -> 21.6 us  [the longest x3 21.6 us: body(): got.append(here(lax.ppermute(sent, 'batch', route(k))))]
    slice x10 -> x0, local copies, waits for them, and re-layouts: 1.8 us -> none  [the longest x2 1.37 us: body(): self_cache[0]]
    select_n x2 -> x0, other arithmetic: 1.45 us -> none  [the longest x1 1.45 us: extend(): return jnp.where(alive[:, None, None], grown, jnp.zeros_like(older))]
  transfers between devices with their start and end apart: 7 -> 5, of which waited for: 4 -> 1; matrix products, arithmetic and copies ran while one was open for 6% -> 0% of each run, Pallas kernels for 0% -> 2%
where the time goes in v1:
time: 105 us; the launch traced here: 104 us
  starting transfers between devices  60 us (57%)
  waiting for transfers between devices  21.6 us (21%)
  Pallas kernels  10 us (10%)
  blocking collectives  9.31 us (9%)
  local copies, waits for them, and re-layouts  2.46 us (2%)
    ppermute x1, starting transfers between devices, body(): lax.ppermute(partial, 'mp', [(i, (i + 1) % cores) for i in range(cores)])  43.4 us
    ppermute x3, waiting for transfers between devices, body(): got.append(here(lax.ppermute(sent, 'batch', route(k))))  21.6 us
    all_to_all x1, blocking collectives, exchange(): lax.all_to_all(chunks, 'batch', split_axis=0, concat_axis=0, tiled=True,...  9.31 us
    ppermute x3, starting transfers between devices, body(): got.append(here(lax.ppermute(sent, 'batch', route(k))))  8.49 us
    all_to_all x1, starting transfers between devices, exchange(): lax.all_to_all(chunks, 'batch', split_axis=0, concat_axis=0, tiled=True,...  8.17 us
    pallas_call x1, Pallas kernels, body(): pl.pallas_call(functools.partial(cross_attention, count=count), in_specs=...  3.93 us
    unnamed x18, local copies, waits for them, and re-layouts  2.46 us
    pallas_call x1, Pallas kernels, body(): pl.pallas_call(self_attention, in_specs=[SMEM, VMEM, VMEM, HBM], out_spec...  2.36 us
  transfers between devices with their start and end apart: 5, of which 1 were waited for; matrix products, arithmetic and copies ran while one was open for 0% of the time, Pallas kernels for 2%

profile of v1, /device:TPU:33, one launch (start us, length us, event | category | flops | bytes accessed | tf_op | source)
XLA Modules:
  0.0 104.3 jit_solution(17391796292916611131)
XLA Ops:
  0.6 0.0 copy-start
  0.6 1.1 %copy-done = bf16[2,2,128,640]{3,2,1,0:T(8,128)(2,1)S(1)} copy-done((bf16[2,2,128,640]{3,2,1,0:T(8,128)(2,1)S(1)}, bf16[2,2,128,640]{3,2,1,0:T(8,128)(2,1)}, u32[]{:S(2)}) %copy-start) | copy-done | bytes 655384
  1.7 0.7 copy-done.2
  2.4 0.7 copy-done.8
  3.1 0.0 copy-start.6
  3.1 0.0 copy-start.7
  3.1 2.4 %self_attention.1.mine = f32[2,1280]{1,0:T(2,128)S(1)} custom-call(s32[2]{0:T(128)S(1)} %copy-done.8, bf16[3,2,640]{2,1,0:T(2,128)(2,1)S(1)} %copy-done.2, bf16[2,2,128,640]{3,2,1,0:T(8,128)(2,1)S(1)} %copy-done, bf16[640,1280]{1,0:T(8,128)(2,1)} %proj_hbm.2), custom_call_target="tpu_custom_call" | custom-call | tf_op jit(solution)/shard_map/self_attention/pallas_call | solution.py:246
  5.5 43.4 %collective-permute-start = (f32[2,1280]{1,0:T(2,128)S(1)}, f32[2,1280]{1,0:T(2,128)S(1)}, u32[]{:S(2)}, u32[]{:S(2)}) collective-permute-start(f32[2,1280]{1,0:T(2,128)S(1)} %self_attention.1.mine), channel_id=1, source_target_pairs={{0,1},{1,0},{2,3},{3,2},{4,5},{5,4},{6,7},{7,6},{8,9},{9,8},{10,11... | collective-permute-start | bytes 30728 | tf_op jit(solution)/shard_map/ppermute | solution.py:255
  48.9 2.1 %prepare.1 = (bf16[2,256,640]{2,1,0:T(8,128)(2,1)S(1)}, bf16[4,256,640]{2,1,0:T(8,128)(2,1)}) custom-call(s32[1]{0:T(128)} %bitcast.me_hbm.me_ref, s32[2]{0:T(128)} %length.1, s32[2]{0:T(128)} %finished.1, s32[2]{0:T(128)} %new_slot.3, bf16[3,2,640]{2,1,0:T(2,128)(2,1)} %qkv.1, bf16[2,2,128,640]{3,2,1,0:T(8,128)(2,1)} %cache.1), custom_call_target="tpu_custom_call" | custom-call | tf_op jit(solution)/shard_map/prepare/pallas_call | solution.py:234
  51.0 0.0 collective-permute-done.other
  51.0 0.0 copy-done.1
  51.0 0.0 copy-done.3
  51.0 0.0 copy-done.4
  51.0 3.9 %cross_attention.1 = (bf16[2,640]{1,0:T(2,128)(2,1)S(1)}, bf16[4,8,640]{2,1,0:T(8,128)(2,1)S(1)}, bf16[264,640]{1,0:T(8,128)(2,1)}, bf16[264,640]{1,0:T(8,128)(2,1)}, bf16[264,640]{1,0:T(8,128)(2,1)S(1)}) custom-call(s32[1]{0:T(128)} %bitcast.me_hbm.me_ref, s32[2]{0:T(128)S(1)} %copy-done.7, s32[2]{0:T(128)S(1)} %copy-done.6, bf16[2,1280]{1,0:T(2,128)(2,1)S(1)} %copy-done.5, ...), custom_call_target="tpu_custom_call" | custom-call | tf_op jit(solution)/shard_map/cross_attention/pallas_call | solution.py:256
  55.0 9.3 %all_to_all.10.near = bf16[4,8,640]{2,1,0:T(8,128)(2,1)S(1)} all-to-all(bf16[4,8,640]{2,1,0:T(8,128)(2,1)S(1)} %get-tuple-element.12), channel_id=1, replica_groups={{252,254,0,2},{4,6,8,10},{12,14,16,18},{20,22,24,26},{28,30,32,34},{36,..., dimensions={0} | all-to-all | bytes 81920 | tf_op jit(solution)/shard_map/all_to_all | solution.py:223
  64.3 8.2 %all-to-all-start = ((bf16[4,256,640]{2,1,0:T(8,128)(2,1)}), bf16[4,256,640]{2,1,0:T(8,128)(2,1)S(1)}, u32[]{:S(2)}, u32[]{:S(2)}) async-start(bf16[4,256,640]{2,1,0:T(8,128)(2,1)} %get-tuple-element.11), calls=%async_computation | async-start | bytes 2621440 | tf_op jit(solution)/shard_map/all_to_all | solution.py:223
  72.5 1.9 %collective-permute-start.1 = (bf16[264,640]{1,0:T(8,128)(2,1)}, bf16[264,640]{1,0:T(8,128)(2,1)S(1)}, u32[]{:S(2)}, u32[]{:S(2)}) collective-permute-start(bf16[264,640]{1,0:T(8,128)(2,1)} %get-tuple-element.13), channel_id=1, source_target_pairs={{0,250},{2,4},{4,254},{6,0},{8,2},{10,12},{12,6},{14,8},{16,10},{1... | collective-permute-start | bytes 1013768 | tf_op jit(solution)/shard_map/ppermute | solution.py:267
  74.4 3.4 %collective-permute-start.2 = (bf16[264,640]{1,0:T(8,128)(2,1)}, bf16[264,640]{1,0:T(8,128)(2,1)S(1)}, u32[]{:S(2)}, u32[]{:S(2)}) collective-permute-start(bf16[264,640]{1,0:T(8,128)(2,1)} %get-tuple-element.14), channel_id=1, source_target_pairs={{0,4},{2,6},{4,0},{6,2},{8,12},{10,14},{12,8},{14,10},{16,20},{18,... | collective-permute-start | bytes 1013768 | tf_op jit(solution)/shard_map/ppermute | solution.py:267
  77.8 3.2 %collective-permute-start.3 = (bf16[264,640]{1,0:T(8,128)(2,1)S(1)}, bf16[264,640]{1,0:T(8,128)(2,1)S(1)}, u32[]{:S(2)}, u32[]{:S(2)}) collective-permute-start(bf16[264,640]{1,0:T(8,128)(2,1)S(1)} %get-tuple-element.15), channel_id=1, source_target_pairs={{0,6},{2,8},{4,2},{6,12},{8,14},{10,16},{12,10},{14,20},{16,22},{1... | collective-permute-start | bytes 1013768 | tf_op jit(solution)/shard_map/ppermute | solution.py:267
  81.0 21.6 %collective-permute-done.1.got1 = bf16[264,640]{1,0:T(8,128)(2,1)S(1)} collective-permute-done((bf16[264,640]{1,0:T(8,128)(2,1)}, bf16[264,640]{1,0:T(8,128)(2,1)S(1)}, u32[]{:S(2)}, u32[]{:S(2)}) %collective-permute-start.1) | collective-permute-done | bytes 337952 | tf_op jit(solution)/shard_map/ppermute | solution.py:267
  102.6 0.0 collective-permute-done.2.got2
  102.6 0.0 collective-permute-done.3.got3
  102.6 0.0 all-to-all-done.inner
  102.6 1.6 %assemble.1 = (bf16[2,2,128,640]{3,2,1,0:T(8,128)(2,1)}, bf16[2,640]{1,0:T(2,128)(2,1)}) custom-call(s32[1]{0:T(128)} %bitcast.me_hbm.me_ref, s32[2]{0:T(128)S(1)} %copy-done.6, bf16[2,256,640]{2,1,0:T(8,128)(2,1)S(1)} %get-tuple-element.9.updated, bf16[2,640]{1,0:T(2,128)(2,1)S(1)} %get-tuple-element.10.decoded, ...), custom_call_target="tpu_custom_call" | custom-call | tf_op jit(solution)/shard_map/assemble/pallas_call | solution.py:269
  (9 shorter events, 0.0 us)
Async XLA Ops:
  0.6 1.1 %copy-start = (bf16[2,2,128,640]{3,2,1,0:T(8,128)(2,1)S(1)}, bf16[2,2,128,640]{3,2,1,0:T(8,128)(2,1)}, u32[]{:S(2)}) copy-start(bf16[2,2,128,640]{3,2,1,0:T(8,128)(2,1)} %cache.1) | copy-start | bytes 1966084
  1.7 0.7 copy-start.2
  2.4 0.7 copy-start.8
  3.1 47.9 %copy-start.1 = (bf16[2,2,64,640]{3,2,1,0:T(8,128)(2,1)S(1)}, bf16[2,2,64,640]{3,2,1,0:T(8,128)(2,1)}, u32[]{:S(2)}) copy-start(bf16[2,2,64,640]{3,2,1,0:T(8,128)(2,1)} %cross.1) | copy-start | bytes 983044
  3.1 47.9 %copy-start.3 = (f32[1280]{0:T(1024)S(1)}, f32[1280]{0:T(1024)}, u32[]{:S(2)}) copy-start(f32[1280]{0:T(1024)} %gain.1) | copy-start | bytes 15364
  3.1 47.9 %copy-start.4 = (f32[1280]{0:T(1024)S(1)}, f32[1280]{0:T(1024)}, u32[]{:S(2)}) copy-start(f32[1280]{0:T(1024)} %bias.1) | copy-start | bytes 15364
  3.1 47.9 %copy-start.5 = (bf16[2,1280]{1,0:T(2,128)(2,1)S(1)}, bf16[2,1280]{1,0:T(2,128)(2,1)}, u32[]{:S(2)}) copy-start(bf16[2,1280]{1,0:T(2,128)(2,1)} %hidden.1) | copy-start | bytes 15364
  3.1 47.9 %copy-start.6 = (s32[2]{0:T(128)S(1)}, s32[2]{0:T(128)}, u32[]{:S(2)}) copy-start(s32[2]{0:T(128)} %new_slot.3) | copy-start | bytes 28
  3.1 47.9 %copy-start.7 = (s32[2]{0:T(128)S(1)}, s32[2]{0:T(128)}, u32[]{:S(2)}) copy-start(s32[2]{0:T(128)} %finished.1) | copy-start | bytes 28
  5.5 45.5 %collective-permute-start = (f32[2,1280]{1,0:T(2,128)S(1)}, f32[2,1280]{1,0:T(2,128)S(1)}, u32[]{:S(2)}, u32[]{:S(2)}) collective-permute-start(f32[2,1280]{1,0:T(2,128)S(1)} %self_attention.1.mine), channel_id=1, source_target_pairs={{0,1},{1,0},{2,3},{3,2},{4,5},{5,4},{6,7},{7,6},{8,9},{9,8},{10,11... | collective-permute-start | bytes 30728 | tf_op jit(solution)/shard_map/ppermute | solution.py:255
  64.3 38.3 %all-to-all-start = ((bf16[4,256,640]{2,1,0:T(8,128)(2,1)}), bf16[4,256,640]{2,1,0:T(8,128)(2,1)S(1)}, u32[]{:S(2)}, u32[]{:S(2)}) async-start(bf16[4,256,640]{2,1,0:T(8,128)(2,1)} %get-tuple-element.11), calls=%async_computation | async-start | bytes 2621440 | tf_op jit(solution)/shard_map/all_to_all | solution.py:223
  72.5 30.1 %collective-permute-start.1 = (bf16[264,640]{1,0:T(8,128)(2,1)}, bf16[264,640]{1,0:T(8,128)(2,1)S(1)}, u32[]{:S(2)}, u32[]{:S(2)}) collective-permute-start(bf16[264,640]{1,0:T(8,128)(2,1)} %get-tuple-element.13), channel_id=1, source_target_pairs={{0,250},{2,4},{4,254},{6,0},{8,2},{10,12},{12,6},{14,8},{16,10},{1... | collective-permute-start | bytes 1013768 | tf_op jit(solution)/shard_map/ppermute | solution.py:267
  74.4 28.2 %collective-permute-start.2 = (bf16[264,640]{1,0:T(8,128)(2,1)}, bf16[264,640]{1,0:T(8,128)(2,1)S(1)}, u32[]{:S(2)}, u32[]{:S(2)}) collective-permute-start(bf16[264,640]{1,0:T(8,128)(2,1)} %get-tuple-element.14), channel_id=1, source_target_pairs={{0,4},{2,6},{4,0},{6,2},{8,12},{10,14},{12,8},{14,10},{16,20},{18,... | collective-permute-start | bytes 1013768 | tf_op jit(solution)/shard_map/ppermute | solution.py:267
  77.8 24.8 %collective-permute-start.3 = (bf16[264,640]{1,0:T(8,128)(2,1)S(1)}, bf16[264,640]{1,0:T(8,128)(2,1)S(1)}, u32[]{:S(2)}, u32[]{:S(2)}) collective-permute-start(bf16[264,640]{1,0:T(8,128)(2,1)S(1)} %get-tuple-element.15), channel_id=1, source_target_pairs={{0,6},{2,8},{4,2},{6,12},{8,14},{10,16},{12,10},{14,20},{16,22},{1... | collective-permute-start | bytes 1013768 | tf_op jit(solution)/shard_map/ppermute | solution.py:267

commit v2 on v1

--- a/solution.py
+++ b/solution.py
@@ -36,25 +36,26 @@
 
 
 def prepare(me_hbm, length_hbm, finished_hbm, slot_hbm, qkv_hbm, cache_hbm, *rest, count):
-    updated, chunks, me_ref, length, finished, new_slot, qkv, cache, sems = rest
-    pairs = (
-        (cache_hbm, cache),
+    updated, kept, chunks, me_ref, length, finished, new_slot, qkv, cache, sems = rest
+    spans, slots, width = cache.shape[1:]
+    pairs = [(cache_hbm.at[:, j], cache.at[:, j]) for j in range(spans)]
+    pairs += [
         (me_hbm, me_ref),
         (length_hbm, length),
         (finished_hbm, finished),
         (slot_hbm, new_slot),
         (qkv_hbm, qkv),
-    )
+    ]
     copies = [pltpu.make_async_copy(a, b, sems.at[i]) for i, (a, b) in enumerate(pairs)]
-    for copy in copies:
+    for copy in copies[spans:] + copies[:spans]:
         copy.start()
-    for copy in copies:
+    for copy in copies[spans:]:
         copy.wait()
-    spans, slots, width = cache.shape[1:]
     me = me_ref[0]
     position = lax.broadcasted_iota(jnp.int32, (slots, width), 0)
     sends = []
     for j in range(spans):
+        copies[j].wait()
         limit = jnp.where(finished[j] == 0, length[j], -1)
         for a in range(2):
             older = cache[a, j].astype(jnp.float32)
@@ -62,6 +63,8 @@
             grown = jnp.where(position < limit, older, jnp.where(position == limit, fresh, 0.0))
             updated[j, a * slots : (a + 1) * slots] = grown.astype(jnp.bfloat16)
         plan = moves(new_slot, me, spans, count, j)
+        mark = jnp.where(plan.stays, plan.local + 1, 0).astype(jnp.float32)
+        kept[j] = jnp.full(kept.shape[1:], mark, jnp.float32)
         send = pltpu.make_async_copy(updated.at[j], chunks.at[plan.place], sems.at[j])
         sends.append((plan.inside, send))
 
@@ -131,10 +134,8 @@
 
 
 def cross_attention(
-    me_ref, finished, new_slot, hidden, mine, other, gain, bias, cross, updated, proj_hbm, decoded, near, far1, far2, far3, proj, sem, *, count
+    me_ref, finished, new_slot, hidden, mine, other, gain, bias, cross, updated, proj, decoded, near, far1, far2, far3, *, count
 ):
-    copy = pltpu.make_async_copy(proj_hbm, proj, sem)
-    copy.start()
     spans, _, width = cross.shape[1:]
     rows = updated.shape[1]
     heads = -(-(width // HEAD_DIM) // 8) * 8
@@ -152,7 +153,6 @@
     centre = jnp.mean(resid, axis=1, keepdims=True)
     spread = jnp.mean((resid - centre) ** 2, axis=1, keepdims=True)
     normed = ((resid - centre) * lax.rsqrt(spread + 1e-05) * gain[...][None] + bias[...][None]).astype(jnp.bfloat16)
-    copy.wait()
     queries = jnp.dot(normed, proj[...], preferred_element_type=jnp.float32).astype(jnp.bfloat16).astype(jnp.float32)
     results = []
     for j in range(spans):
@@ -175,31 +175,33 @@
         near[x] = tile_of(*pick(plans, [p.inside & (p.place == x) for p in plans], results))
 
 
-def assemble(me_ref, new_slot, updated, decoded, inner, near, got1, got2, got3, moved, moved_out, *, count):
+def assemble(kept, updated, decoded, inner, near, got1, got2, got3, moved, moved_out):
     spans, slots, width = moved.shape[1:]
     rows = 2 * slots
-    me = me_ref[0]
-    sources = []
-    tails = [(near[x], inner.at[x]) for x in range(RING)] + [(got[rows:], got) for got in (got1, got2, got3)]
-    for tile, block in tails:
-        tile = tile.astype(jnp.float32)
-        sources.append((jnp.max(tile[1:, :128]), block, tile[:1]))
-    for j in range(spans):
-        p = moves(new_slot, me, spans, count, j)
-        mark = jnp.where(p.stays, p.local + 1, 0).astype(jnp.float32)
-        sources.append((mark, updated.at[j], decoded[j : j + 1].astype(jnp.float32)))
+    tails = [near[x].astype(jnp.float32) for x in range(RING)]
+    tails += [got[rows:].astype(jnp.float32) for got in (got1, got2, got3)]
+    blocks = [inner.at[x] for x in range(RING)] + [got1, got2, got3] + [updated.at[j] for j in range(spans)]
+    found, lines = [], []
     for l in range(spans):
+        source = jnp.zeros((1, 128), jnp.float32)
         row = jnp.zeros((1, width), jnp.float32)
-        for mark, block, line in sources:
-            chosen = mark == l + 1
-            row = jnp.where(chosen, line, row)
-
-            @pl.when(chosen)
+        for i, tile in enumerate(tails):
+            source = jnp.where(tile[1:2, :128] == l + 1, float(i), source)
+            row = jnp.where(tile[1:2] == l + 1, tile[:1], row)
+        for j in range(spans):
+            source = jnp.where(kept[j, :1, :128] == l + 1, float(len(tails) + j), source)
+            row = jnp.where(kept[j, :1] == l + 1, decoded[j : j + 1].astype(jnp.float32), row)
+        source = jnp.max(source).astype(jnp.int32)
+        found.append(source)
+        lines.append(row)
+    moved_out[...] = jnp.concatenate(lines, axis=0).astype(jnp.bfloat16)
+    for l, source in enumerate(found):
+        for i, block in enumerate(blocks):
+
+            @pl.when(source == i)
             def _(block=block, l=l):
                 for a in range(2):
                     moved[a, l] = block[a * slots : (a + 1) * slots]
-
-        moved_out[l : l + 1] = row.astype(jnp.bfloat16)
 
 
 def here(array):
@@ -231,14 +233,18 @@
         return pairs
 
     block = pltpu.VMEM((rows + TAIL, width), bf16)
-    updated, chunks = pl.pallas_call(
+    updated, kept, chunks = pl.pallas_call(
         functools.partial(prepare, count=count),
         in_specs=[HBM] * 6,
-        out_specs=[VMEM, HBM],
-        out_shape=[pltpu.VMEM((spans, rows, width), bf16), pltpu.HBM((RING, rows, width), bf16)],
+        out_specs=[VMEM, VMEM, HBM],
+        out_shape=[
+            pltpu.VMEM((spans, rows, width), bf16),
+            pltpu.VMEM((spans, TAIL, width), jnp.float32),
+            pltpu.HBM((RING, rows, width), bf16),
+        ],
         scratch_shapes=[pltpu.SMEM((1,), jnp.int32)]
         + [pltpu.SMEM((spans,), jnp.int32)] * 3
-        + [pltpu.VMEM(token_qkv.shape, bf16), pltpu.VMEM(self_cache.shape, bf16), pltpu.SemaphoreType.DMA((6,))],
+        + [pltpu.VMEM(token_qkv.shape, bf16), pltpu.VMEM(self_cache.shape, bf16), pltpu.SemaphoreType.DMA((5 + spans,))],
         compiler_params=LIMIT,
         name="prepare",
     )(*map(there, (me, cache_len, finished, new_slot, token_qkv, self_cache)))
@@ -255,25 +261,24 @@
     other = here(lax.ppermute(partial, "mp", [(i, (i + 1) % cores) for i in range(cores)]))
     decoded, near, *far = pl.pallas_call(
         functools.partial(cross_attention, count=count),
-        in_specs=[SMEM] * 3 + [VMEM] * 7 + [HBM],
+        in_specs=[SMEM] * 3 + [VMEM] * 8,
         out_specs=[VMEM] * 5,
         out_shape=[pltpu.VMEM((spans, width), bf16), pltpu.VMEM((RING, TAIL, width), bf16)] + [block] * 3,
-        scratch_shapes=[pltpu.VMEM(query_proj.shape, bf16), pltpu.SemaphoreType.DMA],
         compiler_params=LIMIT,
         name="cross_attention",
-    )(me, finished, new_slot, hidden, here(partial), other, ln_gain, ln_bias, cross_kv, here(updated), there(query_proj))
+    )(me, finished, new_slot, hidden, here(partial), other, ln_gain, ln_bias, cross_kv, here(updated), here(query_proj))
     got = []
     for k, sent in enumerate(far, 1):
         got.append(here(lax.ppermute(sent, "batch", route(k))))
     close = exchange(near)
     return pl.pallas_call(
-        functools.partial(assemble, count=count),
-        in_specs=[SMEM] * 2 + [VMEM] * 7,
+        assemble,
+        in_specs=[VMEM] * 8,
         out_specs=[VMEM] * 2,
         out_shape=[jax.ShapeDtypeStruct(self_cache.shape, bf16), jax.ShapeDtypeStruct((spans, width), bf16)],
         compiler_params=LIMIT,
         name="assemble",
-    )(me, new_slot, here(updated), here(decoded), inner, close, *got)
+    )(here(kept), here(updated), here(decoded), inner, close, *got)
 
 
 def solution(mesh):

time: 105 us -> 104 us (level)
  Pallas kernels: 10 us -> 8.19 us
  local copies, waits for them, and re-layouts: 2.46 us -> 3.89 us
    unnamed x18 -> x20, local copies, waits for them, and re-layouts: 2.46 us -> 3.89 us
    pallas_call x1, Pallas kernels: 3.93 us -> 2.72 us  [body(): pl.pallas_call(functools.partial(cross_attention, count=count), in_specs=...]
where the time goes in v2:
time: 104 us
  starting transfers between devices  60 us (58%)
  waiting for transfers between devices  21.6 us (21%)
  blocking collectives  9.3 us (9%)
  Pallas kernels  8.19 us (8%)
  local copies, waits for them, and re-layouts  3.89 us (4%)
    ppermute x1, starting transfers between devices, body(): lax.ppermute(partial, 'mp', [(i, (i + 1) % cores) for i in range(cores)])  43.4 us
    ppermute x3, waiting for transfers between devices, body(): got.append(here(lax.ppermute(sent, 'batch', route(k))))  21.6 us
    all_to_all x1, blocking collectives, exchange(): lax.all_to_all(chunks, 'batch', split_axis=0, concat_axis=0, tiled=True,...  9.3 us
    ppermute x3, starting transfers between devices, body(): got.append(here(lax.ppermute(sent, 'batch', route(k))))  8.49 us
    all_to_all x1, starting transfers between devices, exchange(): lax.all_to_all(chunks, 'batch', split_axis=0, concat_axis=0, tiled=True,...  8.17 us
    unnamed x20, local copies, waits for them, and re-layouts  3.89 us
    pallas_call x1, Pallas kernels, body(): pl.pallas_call(functools.partial(cross_attention, count=count), in_specs=...  2.72 us
    pallas_call x1, Pallas kernels, body(): pl.pallas_call(self_attention, in_specs=[SMEM, VMEM, VMEM, HBM], out_spec...  2.36 us
  transfers between devices with their start and end apart: 5, of which 1 were waited for; matrix products, arithmetic and copies ran while one was open for 0% of the time, Pallas kernels for 2%

profile of v2, /device:TPU:33, one launch (start us, length us, event | category | flops | bytes accessed | tf_op | source)
XLA Modules:
  0.0 103.8 jit_solution(3199722129899583009)
XLA Ops:
  0.6 0.0 copy-start
  0.6 1.1 %copy-done = bf16[2,2,128,640]{3,2,1,0:T(8,128)(2,1)S(1)} copy-done((bf16[2,2,128,640]{3,2,1,0:T(8,128)(2,1)S(1)}, bf16[2,2,128,640]{3,2,1,0:T(8,128)(2,1)}, u32[]{:S(2)}) %copy-start) | copy-done | bytes 655384
  1.7 0.7 copy-done.3
  2.4 0.7 copy-done.9
  3.1 0.0 copy-start.7
  3.1 0.0 copy-start.8
  3.1 2.4 %self_attention.1.mine = f32[2,1280]{1,0:T(2,128)S(1)} custom-call(s32[2]{0:T(128)S(1)} %copy-done.9, bf16[3,2,640]{2,1,0:T(2,128)(2,1)S(1)} %copy-done.3, bf16[2,2,128,640]{3,2,1,0:T(8,128)(2,1)S(1)} %copy-done, bf16[640,1280]{1,0:T(8,128)(2,1)} %proj_hbm.1), custom_call_target="tpu_custom_call" | custom-call | tf_op jit(solution)/shard_map/self_attention/pallas_call | solution.py:252
  5.5 43.4 %collective-permute-start = (f32[2,1280]{1,0:T(2,128)S(1)}, f32[2,1280]{1,0:T(2,128)S(1)}, u32[]{:S(2)}, u32[]{:S(2)}) collective-permute-start(f32[2,1280]{1,0:T(2,128)S(1)} %self_attention.1.mine), channel_id=1, source_target_pairs={{0,1},{1,0},{2,3},{3,2},{4,5},{5,4},{6,7},{7,6},{8,9},{9,8},{10,11... | collective-permute-start | bytes 30728 | tf_op jit(solution)/shard_map/ppermute | solution.py:261
  48.9 2.0 %prepare.1 = (bf16[2,256,640]{2,1,0:T(8,128)(2,1)S(1)}, f32[2,8,640]{2,1,0:T(8,128)S(1)}, bf16[4,256,640]{2,1,0:T(8,128)(2,1)}) custom-call(s32[1]{0:T(128)} %bitcast.me_hbm.me_ref, s32[2]{0:T(128)} %length.1, s32[2]{0:T(128)} %finished.1, s32[2]{0:T(128)} %new_slot.1, bf16[3,2,640]{2,1,0:T(2,128)(2,1)} %qkv.1, bf16[2,2,128,640]{3,2,1,0:T(8,128)(2,1)} %cache.1), custom_call_target="tpu_custom_call" | custom-call | tf_op jit(solution)/shard_map/prepare/pallas_call | solution.py:236
  50.9 0.0 collective-permute-done.other
  50.9 0.0 copy-done.2
  50.9 0.0 copy-start.1
  50.9 1.4 %copy-done.1 = bf16[1280,640]{1,0:T(8,128)(2,1)S(1)} copy-done((bf16[1280,640]{1,0:T(8,128)(2,1)S(1)}, bf16[1280,640]{1,0:T(8,128)(2,1)}, u32[]{:S(2)}) %copy-start.1) | copy-done | bytes 1638424
  52.4 2.7 %cross_attention.1 = (bf16[2,640]{1,0:T(2,128)(2,1)S(1)}, bf16[4,8,640]{2,1,0:T(8,128)(2,1)S(1)}, bf16[264,640]{1,0:T(8,128)(2,1)}, bf16[264,640]{1,0:T(8,128)(2,1)}, bf16[264,640]{1,0:T(8,128)(2,1)S(1)}) custom-call(s32[1]{0:T(128)} %bitcast.me_hbm.me_ref, s32[2]{0:T(128)S(1)} %copy-done.7, s32[2]{0:T(128)S(1)} %copy-done.8, bf16[2,1280]{1,0:T(2,128)(2,1)S(1)} %copy-done.6, ...), custom_call_target="tpu_custom_call" | custom-call | tf_op jit(solution)/shard_map/cross_attention/pallas_call | solution.py:262
  55.1 9.3 %all_to_all.10.near = bf16[4,8,640]{2,1,0:T(8,128)(2,1)S(1)} all-to-all(bf16[4,8,640]{2,1,0:T(8,128)(2,1)S(1)} %get-tuple-element.14), channel_id=1, replica_groups={{252,254,0,2},{4,6,8,10},{12,14,16,18},{20,22,24,26},{28,30,32,34},{36,..., dimensions={0} | all-to-all | bytes 81920 | tf_op jit(solution)/shard_map/all_to_all | solution.py:225
  64.4 8.2 %all-to-all-start = ((bf16[4,256,640]{2,1,0:T(8,128)(2,1)}), bf16[4,256,640]{2,1,0:T(8,128)(2,1)S(1)}, u32[]{:S(2)}, u32[]{:S(2)}) async-start(bf16[4,256,640]{2,1,0:T(8,128)(2,1)} %get-tuple-element.13), calls=%async_computation | async-start | bytes 2621440 | tf_op jit(solution)/shard_map/all_to_all | solution.py:225
  72.6 1.9 %collective-permute-start.1 = (bf16[264,640]{1,0:T(8,128)(2,1)}, bf16[264,640]{1,0:T(8,128)(2,1)S(1)}, u32[]{:S(2)}, u32[]{:S(2)}) collective-permute-start(bf16[264,640]{1,0:T(8,128)(2,1)} %get-tuple-element.15), channel_id=1, source_target_pairs={{0,250},{2,4},{4,254},{6,0},{8,2},{10,12},{12,6},{14,8},{16,10},{1... | collective-permute-start | bytes 1013768 | tf_op jit(solution)/shard_map/ppermute | solution.py:272
  74.5 3.4 %collective-permute-start.2 = (bf16[264,640]{1,0:T(8,128)(2,1)}, bf16[264,640]{1,0:T(8,128)(2,1)S(1)}, u32[]{:S(2)}, u32[]{:S(2)}) collective-permute-start(bf16[264,640]{1,0:T(8,128)(2,1)} %get-tuple-element.16), channel_id=1, source_target_pairs={{0,4},{2,6},{4,0},{6,2},{8,12},{10,14},{12,8},{14,10},{16,20},{18,... | collective-permute-start | bytes 1013768 | tf_op jit(solution)/shard_map/ppermute | solution.py:272
  77.9 3.2 %collective-permute-start.3 = (bf16[264,640]{1,0:T(8,128)(2,1)S(1)}, bf16[264,640]{1,0:T(8,128)(2,1)S(1)}, u32[]{:S(2)}, u32[]{:S(2)}) collective-permute-start(bf16[264,640]{1,0:T(8,128)(2,1)S(1)} %get-tuple-element.17), channel_id=1, source_target_pairs={{0,6},{2,8},{4,2},{6,12},{8,14},{10,16},{12,10},{14,20},{16,22},{1... | collective-permute-start | bytes 1013768 | tf_op jit(solution)/shard_map/ppermute | solution.py:272
  81.1 21.6 %collective-permute-done.1.got1 = bf16[264,640]{1,0:T(8,128)(2,1)S(1)} collective-permute-done((bf16[264,640]{1,0:T(8,128)(2,1)}, bf16[264,640]{1,0:T(8,128)(2,1)S(1)}, u32[]{:S(2)}, u32[]{:S(2)}) %collective-permute-start.1) | collective-permute-done | bytes 337952 | tf_op jit(solution)/shard_map/ppermute | solution.py:272
  102.7 0.0 collective-permute-done.2.got2
  102.7 0.0 collective-permute-done.3.got3
  102.7 0.0 all-to-all-done.inner
  102.7 1.1 %assemble.1 = (bf16[2,2,128,640]{3,2,1,0:T(8,128)(2,1)}, bf16[2,640]{1,0:T(2,128)(2,1)}) custom-call(f32[2,8,640]{2,1,0:T(8,128)S(1)} %get-tuple-element.10.kept, bf16[2,256,640]{2,1,0:T(8,128)(2,1)S(1)} %get-tuple-element.11.updated, bf16[2,640]{1,0:T(2,128)(2,1)S(1)} %get-tuple-element.12.decoded, bf16[4,256,640]{2,1,0:T(8,128)(2,1)S(1)} %all-to-all-done.inner, ...), custom_call_target="tpu_custom_call" | custom-call | tf_op jit(solution)/shard_map/assemble/pallas_call | solution.py:274
  (11 shorter events, 0.0 us)
Async XLA Ops:
  0.6 1.1 %copy-start = (bf16[2,2,128,640]{3,2,1,0:T(8,128)(2,1)S(1)}, bf16[2,2,128,640]{3,2,1,0:T(8,128)(2,1)}, u32[]{:S(2)}) copy-start(bf16[2,2,128,640]{3,2,1,0:T(8,128)(2,1)} %cache.1) | copy-start | bytes 1966084
  1.7 0.7 copy-start.3
  2.4 0.7 copy-start.9
  3.1 47.8 %copy-start.2 = (bf16[2,2,64,640]{3,2,1,0:T(8,128)(2,1)S(1)}, bf16[2,2,64,640]{3,2,1,0:T(8,128)(2,1)}, u32[]{:S(2)}) copy-start(bf16[2,2,64,640]{3,2,1,0:T(8,128)(2,1)} %cross.1) | copy-start | bytes 983044
  3.1 47.8 %copy-start.4 = (f32[1280]{0:T(1024)S(1)}, f32[1280]{0:T(1024)}, u32[]{:S(2)}) copy-start(f32[1280]{0:T(1024)} %gain.1) | copy-start | bytes 15364
  3.1 47.8 %copy-start.5 = (f32[1280]{0:T(1024)S(1)}, f32[1280]{0:T(1024)}, u32[]{:S(2)}) copy-start(f32[1280]{0:T(1024)} %bias.1) | copy-start | bytes 15364
  3.1 47.8 %copy-start.6 = (bf16[2,1280]{1,0:T(2,128)(2,1)S(1)}, bf16[2,1280]{1,0:T(2,128)(2,1)}, u32[]{:S(2)}) copy-start(bf16[2,1280]{1,0:T(2,128)(2,1)} %hidden.1) | copy-start | bytes 15364
  3.1 47.8 %copy-start.7 = (s32[2]{0:T(128)S(1)}, s32[2]{0:T(128)}, u32[]{:S(2)}) copy-start(s32[2]{0:T(128)} %finished.1) | copy-start | bytes 28
  3.1 47.8 %copy-start.8 = (s32[2]{0:T(128)S(1)}, s32[2]{0:T(128)}, u32[]{:S(2)}) copy-start(s32[2]{0:T(128)} %new_slot.1) | copy-start | bytes 28
  5.5 45.4 %collective-permute-start = (f32[2,1280]{1,0:T(2,128)S(1)}, f32[2,1280]{1,0:T(2,128)S(1)}, u32[]{:S(2)}, u32[]{:S(2)}) collective-permute-start(f32[2,1280]{1,0:T(2,128)S(1)} %self_attention.1.mine), channel_id=1, source_target_pairs={{0,1},{1,0},{2,3},{3,2},{4,5},{5,4},{6,7},{7,6},{8,9},{9,8},{10,11... | collective-permute-start | bytes 30728 | tf_op jit(solution)/shard_map/ppermute | solution.py:261
  50.9 1.4 %copy-start.1 = (bf16[1280,640]{1,0:T(8,128)(2,1)S(1)}, bf16[1280,640]{1,0:T(8,128)(2,1)}, u32[]{:S(2)}) copy-start(bf16[1280,640]{1,0:T(8,128)(2,1)} %proj.1) | copy-start | bytes 4915204
  64.4 38.3 %all-to-all-start = ((bf16[4,256,640]{2,1,0:T(8,128)(2,1)}), bf16[4,256,640]{2,1,0:T(8,128)(2,1)S(1)}, u32[]{:S(2)}, u32[]{:S(2)}) async-start(bf16[4,256,640]{2,1,0:T(8,128)(2,1)} %get-tuple-element.13), calls=%async_computation | async-start | bytes 2621440 | tf_op jit(solution)/shard_map/all_to_all | solution.py:225
  72.6 30.1 %collective-permute-start.1 = (bf16[264,640]{1,0:T(8,128)(2,1)}, bf16[264,640]{1,0:T(8,128)(2,1)S(1)}, u32[]{:S(2)}, u32[]{:S(2)}) collective-permute-start(bf16[264,640]{1,0:T(8,128)(2,1)} %get-tuple-element.15), channel_id=1, source_target_pairs={{0,250},{2,4},{4,254},{6,0},{8,2},{10,12},{12,6},{14,8},{16,10},{1... | collective-permute-start | bytes 1013768 | tf_op jit(solution)/shard_map/ppermute | solution.py:272
  74.5 28.2 %collective-permute-start.2 = (bf16[264,640]{1,0:T(8,128)(2,1)}, bf16[264,640]{1,0:T(8,128)(2,1)S(1)}, u32[]{:S(2)}, u32[]{:S(2)}) collective-permute-start(bf16[264,640]{1,0:T(8,128)(2,1)} %get-tuple-element.16), channel_id=1, source_target_pairs={{0,4},{2,6},{4,0},{6,2},{8,12},{10,14},{12,8},{14,10},{16,20},{18,... | collective-permute-start | bytes 1013768 | tf_op jit(solution)/shard_map/ppermute | solution.py:272
  77.9 24.8 %collective-permute-start.3 = (bf16[264,640]{1,0:T(8,128)(2,1)S(1)}, bf16[264,640]{1,0:T(8,128)(2,1)S(1)}, u32[]{:S(2)}, u32[]{:S(2)}) collective-permute-start(bf16[264,640]{1,0:T(8,128)(2,1)S(1)} %get-tuple-element.17), channel_id=1, source_target_pairs={{0,6},{2,8},{4,2},{6,12},{8,14},{10,16},{12,10},{14,20},{16,22},{1... | collective-permute-start | bytes 1013768 | tf_op jit(solution)/shard_map/ppermute | solution.py:272

commit v3 on v2

--- a/solution.py
+++ b/solution.py
@@ -57,20 +57,21 @@
     for j in range(spans):
         copies[j].wait()
         limit = jnp.where(finished[j] == 0, length[j], -1)
+        plan = moves(new_slot, me, spans, count, j)
+        mark = jnp.where(plan.stays, plan.local + 1, 0).astype(jnp.float32)
+        kept[j] = jnp.full(kept.shape[1:], mark, jnp.float32)
         for a in range(2):
             older = cache[a, j].astype(jnp.float32)
             fresh = qkv[a + 1, j : j + 1].astype(jnp.float32)
             grown = jnp.where(position < limit, older, jnp.where(position == limit, fresh, 0.0))
-            updated[j, a * slots : (a + 1) * slots] = grown.astype(jnp.bfloat16)
-        plan = moves(new_slot, me, spans, count, j)
-        mark = jnp.where(plan.stays, plan.local + 1, 0).astype(jnp.float32)
-        kept[j] = jnp.full(kept.shape[1:], mark, jnp.float32)
-        send = pltpu.make_async_copy(updated.at[j], chunks.at[plan.place], sems.at[j])
-        sends.append((plan.inside, send))
-
-        @pl.when(plan.inside)
-        def _(send=send):
-            send.start()
+            half = pl.ds(a * slots, slots)
+            updated[j, half] = grown.astype(jnp.bfloat16)
+            send = pltpu.make_async_copy(updated.at[j, half], chunks.at[plan.place, half], sems.at[len(copies) + len(sends)])
+            sends.append((plan.inside, send))
+
+            @pl.when(plan.inside)
+            def _(send=send):
+                send.start()
 
     for inside, send in sends:
 
@@ -244,7 +245,7 @@
         ],
         scratch_shapes=[pltpu.SMEM((1,), jnp.int32)]
         + [pltpu.SMEM((spans,), jnp.int32)] * 3
-        + [pltpu.VMEM(token_qkv.shape, bf16), pltpu.VMEM(self_cache.shape, bf16), pltpu.SemaphoreType.DMA((5 + spans,))],
+        + [pltpu.VMEM(token_qkv.shape, bf16), pltpu.VMEM(self_cache.shape, bf16), pltpu.SemaphoreType.DMA((5 + 3 * spans,))],
         compiler_params=LIMIT,
         name="prepare",
     )(*map(there, (me, cache_len, finished, new_slot, token_qkv, self_cache)))

time: 104 us -> 104 us (level)
  no operation moved by 1% of the time
where the time goes in v3:
time: 104 us
  starting transfers between devices  60 us (58%)
  waiting for transfers between devices  21.6 us (21%)
  blocking collectives  9.34 us (9%)
  Pallas kernels  8.18 us (8%)
  local copies, waits for them, and re-layouts  3.89 us (4%)
    ppermute x1, starting transfers between devices, body(): lax.ppermute(partial, 'mp', [(i, (i + 1) % cores) for i in range(cores)])  43.4 us
    ppermute x3, waiting for transfers between devices, body(): got.append(here(lax.ppermute(sent, 'batch', route(k))))  21.6 us
    all_to_all x1, blocking collectives, exchange(): lax.all_to_all(chunks, 'batch', split_axis=0, concat_axis=0, tiled=True,...  9.34 us
    ppermute x3, starting transfers between devices, body(): got.append(here(lax.ppermute(sent, 'batch', route(k))))  8.49 us
    all_to_all x1, starting transfers between devices, exchange(): lax.all_to_all(chunks, 'batch', split_axis=0, concat_axis=0, tiled=True,...  8.17 us
    unnamed x20, local copies, waits for them, and re-layouts  3.89 us
    pallas_call x1, Pallas kernels, body(): pl.pallas_call(functools.partial(cross_attention, count=count), in_specs=...  2.72 us
    pallas_call x1, Pallas kernels, body(): pl.pallas_call(self_attention, in_specs=[SMEM, VMEM, VMEM, HBM], out_spec...  2.36 us
  transfers between devices with their start and end apart: 5, of which 1 were waited for; matrix products, arithmetic and copies ran while one was open for 0% of the time, Pallas kernels for 2%

profile of v3, /device:TPU:33, one launch (start us, length us, event | category | flops | bytes accessed | tf_op | source)
XLA Modules:
  0.0 103.9 jit_solution(237915163565899119)
XLA Ops:
  0.6 0.0 copy-start
  0.6 1.1 %copy-done = bf16[2,2,128,640]{3,2,1,0:T(8,128)(2,1)S(1)} copy-done((bf16[2,2,128,640]{3,2,1,0:T(8,128)(2,1)S(1)}, bf16[2,2,128,640]{3,2,1,0:T(8,128)(2,1)}, u32[]{:S(2)}) %copy-start) | copy-done | bytes 655384
  1.7 0.7 copy-done.3
  2.4 0.7 copy-done.9
  3.1 0.0 copy-start.7
  3.1 0.0 copy-start.8
  3.1 2.4 %self_attention.1.mine = f32[2,1280]{1,0:T(2,128)S(1)} custom-call(s32[2]{0:T(128)S(1)} %copy-done.9, bf16[3,2,640]{2,1,0:T(2,128)(2,1)S(1)} %copy-done.3, bf16[2,2,128,640]{3,2,1,0:T(8,128)(2,1)S(1)} %copy-done, bf16[640,1280]{1,0:T(8,128)(2,1)} %proj_hbm.1), custom_call_target="tpu_custom_call" | custom-call | tf_op jit(solution)/shard_map/self_attention/pallas_call | solution.py:253
  5.5 43.4 %collective-permute-start = (f32[2,1280]{1,0:T(2,128)S(1)}, f32[2,1280]{1,0:T(2,128)S(1)}, u32[]{:S(2)}, u32[]{:S(2)}) collective-permute-start(f32[2,1280]{1,0:T(2,128)S(1)} %self_attention.1.mine), channel_id=1, source_target_pairs={{0,1},{1,0},{2,3},{3,2},{4,5},{5,4},{6,7},{7,6},{8,9},{9,8},{10,11... | collective-permute-start | bytes 30728 | tf_op jit(solution)/shard_map/ppermute | solution.py:262
  48.9 2.0 %prepare.1 = (bf16[2,256,640]{2,1,0:T(8,128)(2,1)S(1)}, f32[2,8,640]{2,1,0:T(8,128)S(1)}, bf16[4,256,640]{2,1,0:T(8,128)(2,1)}) custom-call(s32[1]{0:T(128)} %bitcast.me_hbm.me_ref, s32[2]{0:T(128)} %length.1, s32[2]{0:T(128)} %finished.1, s32[2]{0:T(128)} %new_slot.1, bf16[3,2,640]{2,1,0:T(2,128)(2,1)} %qkv.1, bf16[2,2,128,640]{3,2,1,0:T(8,128)(2,1)} %cache.1), custom_call_target="tpu_custom_call" | custom-call | tf_op jit(solution)/shard_map/prepare/pallas_call | solution.py:237
  50.9 0.0 collective-permute-done.other
  50.9 0.0 copy-done.2
  50.9 0.0 copy-start.1
  50.9 1.4 %copy-done.1 = bf16[1280,640]{1,0:T(8,128)(2,1)S(1)} copy-done((bf16[1280,640]{1,0:T(8,128)(2,1)S(1)}, bf16[1280,640]{1,0:T(8,128)(2,1)}, u32[]{:S(2)}) %copy-start.1) | copy-done | bytes 1638424
  52.4 2.7 %cross_attention.1 = (bf16[2,640]{1,0:T(2,128)(2,1)S(1)}, bf16[4,8,640]{2,1,0:T(8,128)(2,1)S(1)}, bf16[264,640]{1,0:T(8,128)(2,1)}, bf16[264,640]{1,0:T(8,128)(2,1)}, bf16[264,640]{1,0:T(8,128)(2,1)S(1)}) custom-call(s32[1]{0:T(128)} %bitcast.me_hbm.me_ref, s32[2]{0:T(128)S(1)} %copy-done.7, s32[2]{0:T(128)S(1)} %copy-done.8, bf16[2,1280]{1,0:T(2,128)(2,1)S(1)} %copy-done.6, ...), custom_call_target="tpu_custom_call" | custom-call | tf_op jit(solution)/shard_map/cross_attention/pallas_call | solution.py:263
  55.1 9.3 %all_to_all.10.near = bf16[4,8,640]{2,1,0:T(8,128)(2,1)S(1)} all-to-all(bf16[4,8,640]{2,1,0:T(8,128)(2,1)S(1)} %get-tuple-element.14), channel_id=1, replica_groups={{252,254,0,2},{4,6,8,10},{12,14,16,18},{20,22,24,26},{28,30,32,34},{36,..., dimensions={0} | all-to-all | bytes 81920 | tf_op jit(solution)/shard_map/all_to_all | solution.py:226
  64.4 8.2 %all-to-all-start = ((bf16[4,256,640]{2,1,0:T(8,128)(2,1)}), bf16[4,256,640]{2,1,0:T(8,128)(2,1)S(1)}, u32[]{:S(2)}, u32[]{:S(2)}) async-start(bf16[4,256,640]{2,1,0:T(8,128)(2,1)} %get-tuple-element.13), calls=%async_computation | async-start | bytes 2621440 | tf_op jit(solution)/shard_map/all_to_all | solution.py:226
  72.6 1.9 %collective-permute-start.1 = (bf16[264,640]{1,0:T(8,128)(2,1)}, bf16[264,640]{1,0:T(8,128)(2,1)S(1)}, u32[]{:S(2)}, u32[]{:S(2)}) collective-permute-start(bf16[264,640]{1,0:T(8,128)(2,1)} %get-tuple-element.15), channel_id=1, source_target_pairs={{0,250},{2,4},{4,254},{6,0},{8,2},{10,12},{12,6},{14,8},{16,10},{1... | collective-permute-start | bytes 1013768 | tf_op jit(solution)/shard_map/ppermute | solution.py:273
  74.5 3.4 %collective-permute-start.2 = (bf16[264,640]{1,0:T(8,128)(2,1)}, bf16[264,640]{1,0:T(8,128)(2,1)S(1)}, u32[]{:S(2)}, u32[]{:S(2)}) collective-permute-start(bf16[264,640]{1,0:T(8,128)(2,1)} %get-tuple-element.16), channel_id=1, source_target_pairs={{0,4},{2,6},{4,0},{6,2},{8,12},{10,14},{12,8},{14,10},{16,20},{18,... | collective-permute-start | bytes 1013768 | tf_op jit(solution)/shard_map/ppermute | solution.py:273
  77.9 3.2 %collective-permute-start.3 = (bf16[264,640]{1,0:T(8,128)(2,1)S(1)}, bf16[264,640]{1,0:T(8,128)(2,1)S(1)}, u32[]{:S(2)}, u32[]{:S(2)}) collective-permute-start(bf16[264,640]{1,0:T(8,128)(2,1)S(1)} %get-tuple-element.17), channel_id=1, source_target_pairs={{0,6},{2,8},{4,2},{6,12},{8,14},{10,16},{12,10},{14,20},{16,22},{1... | collective-permute-start | bytes 1013768 | tf_op jit(solution)/shard_map/ppermute | solution.py:273
  81.1 21.6 %collective-permute-done.1.got1 = bf16[264,640]{1,0:T(8,128)(2,1)S(1)} collective-permute-done((bf16[264,640]{1,0:T(8,128)(2,1)}, bf16[264,640]{1,0:T(8,128)(2,1)S(1)}, u32[]{:S(2)}, u32[]{:S(2)}) %collective-permute-start.1) | collective-permute-done | bytes 337952 | tf_op jit(solution)/shard_map/ppermute | solution.py:273
  102.7 0.0 collective-permute-done.2.got2
  102.7 0.0 collective-permute-done.3.got3
  102.7 0.0 all-to-all-done.inner
  102.8 1.1 %assemble.1 = (bf16[2,2,128,640]{3,2,1,0:T(8,128)(2,1)}, bf16[2,640]{1,0:T(2,128)(2,1)}) custom-call(f32[2,8,640]{2,1,0:T(8,128)S(1)} %get-tuple-element.10.kept, bf16[2,256,640]{2,1,0:T(8,128)(2,1)S(1)} %get-tuple-element.11.updated, bf16[2,640]{1,0:T(2,128)(2,1)S(1)} %get-tuple-element.12.decoded, bf16[4,256,640]{2,1,0:T(8,128)(2,1)S(1)} %all-to-all-done.inner, ...), custom_call_target="tpu_custom_call" | custom-call | tf_op jit(solution)/shard_map/assemble/pallas_call | solution.py:275
  (11 shorter events, 0.0 us)
Async XLA Ops:
  0.6 1.1 %copy-start = (bf16[2,2,128,640]{3,2,1,0:T(8,128)(2,1)S(1)}, bf16[2,2,128,640]{3,2,1,0:T(8,128)(2,1)}, u32[]{:S(2)}) copy-start(bf16[2,2,128,640]{3,2,1,0:T(8,128)(2,1)} %cache.1) | copy-start | bytes 1966084
  1.7 0.7 copy-start.3
  2.4 0.7 copy-start.9
  3.1 47.8 %copy-start.2 = (bf16[2,2,64,640]{3,2,1,0:T(8,128)(2,1)S(1)}, bf16[2,2,64,640]{3,2,1,0:T(8,128)(2,1)}, u32[]{:S(2)}) copy-start(bf16[2,2,64,640]{3,2,1,0:T(8,128)(2,1)} %cross.1) | copy-start | bytes 983044
  3.1 47.8 %copy-start.4 = (f32[1280]{0:T(1024)S(1)}, f32[1280]{0:T(1024)}, u32[]{:S(2)}) copy-start(f32[1280]{0:T(1024)} %gain.1) | copy-start | bytes 15364
  3.1 47.8 %copy-start.5 = (f32[1280]{0:T(1024)S(1)}, f32[1280]{0:T(1024)}, u32[]{:S(2)}) copy-start(f32[1280]{0:T(1024)} %bias.1) | copy-start | bytes 15364
  3.1 47.8 %copy-start.6 = (bf16[2,1280]{1,0:T(2,128)(2,1)S(1)}, bf16[2,1280]{1,0:T(2,128)(2,1)}, u32[]{:S(2)}) copy-start(bf16[2,1280]{1,0:T(2,128)(2,1)} %hidden.1) | copy-start | bytes 15364
  3.1 47.8 %copy-start.7 = (s32[2]{0:T(128)S(1)}, s32[2]{0:T(128)}, u32[]{:S(2)}) copy-start(s32[2]{0:T(128)} %finished.1) | copy-start | bytes 28
  3.1 47.8 %copy-start.8 = (s32[2]{0:T(128)S(1)}, s32[2]{0:T(128)}, u32[]{:S(2)}) copy-start(s32[2]{0:T(128)} %new_slot.1) | copy-start | bytes 28
  5.5 45.4 %collective-permute-start = (f32[2,1280]{1,0:T(2,128)S(1)}, f32[2,1280]{1,0:T(2,128)S(1)}, u32[]{:S(2)}, u32[]{:S(2)}) collective-permute-start(f32[2,1280]{1,0:T(2,128)S(1)} %self_attention.1.mine), channel_id=1, source_target_pairs={{0,1},{1,0},{2,3},{3,2},{4,5},{5,4},{6,7},{7,6},{8,9},{9,8},{10,11... | collective-permute-start | bytes 30728 | tf_op jit(solution)/shard_map/ppermute | solution.py:262
  50.9 1.4 %copy-start.1 = (bf16[1280,640]{1,0:T(8,128)(2,1)S(1)}, bf16[1280,640]{1,0:T(8,128)(2,1)}, u32[]{:S(2)}) copy-start(bf16[1280,640]{1,0:T(8,128)(2,1)} %proj.1) | copy-start | bytes 4915204
  64.4 38.3 %all-to-all-start = ((bf16[4,256,640]{2,1,0:T(8,128)(2,1)}), bf16[4,256,640]{2,1,0:T(8,128)(2,1)S(1)}, u32[]{:S(2)}, u32[]{:S(2)}) async-start(bf16[4,256,640]{2,1,0:T(8,128)(2,1)} %get-tuple-element.13), calls=%async_computation | async-start | bytes 2621440 | tf_op jit(solution)/shard_map/all_to_all | solution.py:226
  72.6 30.1 %collective-permute-start.1 = (bf16[264,640]{1,0:T(8,128)(2,1)}, bf16[264,640]{1,0:T(8,128)(2,1)S(1)}, u32[]{:S(2)}, u32[]{:S(2)}) collective-permute-start(bf16[264,640]{1,0:T(8,128)(2,1)} %get-tuple-element.15), channel_id=1, source_target_pairs={{0,250},{2,4},{4,254},{6,0},{8,2},{10,12},{12,6},{14,8},{16,10},{1... | collective-permute-start | bytes 1013768 | tf_op jit(solution)/shard_map/ppermute | solution.py:273
  74.5 28.2 %collective-permute-start.2 = (bf16[264,640]{1,0:T(8,128)(2,1)}, bf16[264,640]{1,0:T(8,128)(2,1)S(1)}, u32[]{:S(2)}, u32[]{:S(2)}) collective-permute-start(bf16[264,640]{1,0:T(8,128)(2,1)} %get-tuple-element.16), channel_id=1, source_target_pairs={{0,4},{2,6},{4,0},{6,2},{8,12},{10,14},{12,8},{14,10},{16,20},{18,... | collective-permute-start | bytes 1013768 | tf_op jit(solution)/shard_map/ppermute | solution.py:273
  77.9 24.8 %collective-permute-start.3 = (bf16[264,640]{1,0:T(8,128)(2,1)S(1)}, bf16[264,640]{1,0:T(8,128)(2,1)S(1)}, u32[]{:S(2)}, u32[]{:S(2)}) collective-permute-start(bf16[264,640]{1,0:T(8,128)(2,1)S(1)} %get-tuple-element.17), channel_id=1, source_target_pairs={{0,6},{2,8},{4,2},{6,12},{8,14},{10,16},{12,10},{14,20},{16,22},{1... | collective-permute-start | bytes 1013768 | tf_op jit(solution)/shard_map/ppermute | solution.py:273
